TPU v7x, 256 devices: a whole 4x4x8 slice. The times are simulated.
256 devices in a mesh: rows: 32 (over z, y), cols: 8 (over x, core).
Axes of the slice: x: 4, y: 4, z: 8, core: 2. Of those that a mesh axis runs over, the one named last changes fastest.
Arguments:
- weight_up: bfloat16 [12288, 49152], P('rows', 'cols'), may hold values from -0.109375 to 0.109375
- low_up: bfloat16 [12288, 64], P('rows'), may hold values from -0.0546875 to 0.0546875
- high_up: bfloat16 [64, 49152], P(None, 'cols'), may hold values from -0.75 to 0.75
- norm_train: float32 [12288], P(('rows', 'cols')), may hold values from 0.25 to 1.75
- norm_step: float32 [12288], P(('rows', 'cols')), may hold values from -0.3 to 0.3
Outputs:
- serve_up: bfloat16 [12288, 49152], P(None, ('cols', 'rows'))
- scale_up: float32 [49152], P(('cols', 'rows'))
- serve_norm: bfloat16 [12288], replicated
All inputs are finite; a program needn't handle non-finite values.
Results may differ from a plain program's by a relative error of at most 0.0004.
Values may be sent and summed in bfloat16 or wider, within the bound.
A program may use at most 64 MiB of HBM per device.

v0:
```python
import jax
import jax.numpy as jnp
from jax import lax
from jax.sharding import Mesh
from jax.sharding import PartitionSpec as P

ROWS = ("rows_0", "rows_1")
ROWS_COLS = ("rows_0", "rows_1", "cols_0", "cols_1")
COLS = ("cols_0", "cols_1")
COLS_ROWS = ("cols_0", "cols_1", "rows_0", "rows_1")


mix_rate = 0.5


def copy_for_each(x, axis):
    copies = jnp.broadcast_to(x, (lax.axis_size(axis), *x.shape))
    return lax.all_to_all(copies, axis, split_axis=0, concat_axis=0, tiled=True)


def of_everyone(x, axis):
    return copy_for_each(x, axis).sum(axis=0)


def joined_along(pieces, dim):
    shape = list(pieces.shape[1:])
    shape[dim] *= pieces.shape[0]
    return jnp.moveaxis(pieces, 0, dim).reshape(shape)


def stacked_from(x, axes, sequence):
    pieces = x[None]
    for k in sequence:
        pieces = lax.all_gather(pieces, axes[k], axis=0, tiled=True)
    block = [lax.axis_size(axes[k]) for k in reversed(sequence)]
    pieces = pieces.reshape(*block, *x.shape)
    turned = sorted(range(len(sequence)), key=lambda place: sequence[len(sequence) - 1 - place])
    return pieces.transpose(*turned, *range(len(sequence), pieces.ndim)).reshape(-1, *x.shape)


def gathered_by_axis(x, axes, sequence, dim):
    return joined_along(stacked_from(x, axes, sequence), dim)


def per_device(weight_up, low_up, high_up, norm_train, norm_step):
    fresh_up = weight_up.astype(jnp.float32) + mix_rate * jnp.dot(
        low_up, high_up, preferred_element_type=jnp.float32
    )
    total_up = of_everyone(jnp.sum(fresh_up * fresh_up, axis=0), ROWS)
    scale_up = jnp.sqrt(total_up)
    narrow_up = (fresh_up / scale_up).astype(jnp.bfloat16)
    serve_up = lax.all_to_all(narrow_up, ROWS, split_axis=1, concat_axis=0, tiled=True)
    place = lax.axis_index(ROWS)
    scale_up = lax.dynamic_slice_in_dim(scale_up, place * serve_up.shape[1], serve_up.shape[1])
    serve_norm = gathered_by_axis(
        (norm_train + norm_step).astype(jnp.bfloat16), ROWS_COLS, (1, 0, 2, 3), 0
    )
    return (serve_up, scale_up, serve_norm)


def solution(mesh):
    split = Mesh(mesh.devices.reshape(8, 4, 4, 2), ("rows_0", "rows_1", "cols_0", "cols_1"))
    in_specs = (P(ROWS, COLS), P(ROWS, None), P(None, COLS), P(ROWS_COLS), P(ROWS_COLS))
    out_specs = (P(None, COLS_ROWS), P(COLS_ROWS), P())
    return jax.shard_map(
        per_device, mesh=split, in_specs=in_specs, out_specs=out_specs, check_vma=False
    )
```

profile of v0, /device:TPU:9, one launch (start us, length us, event | category | flops | bytes accessed | tf_op | source)
XLA Modules:
  0.0 197.2 jit_solution(16278709822635123350)
XLA Ops:
  0.6 0.0 copy-start
  0.6 1.1 copy-done
  1.8 8.0 %multiply_reduce_fusion = (f32[6144]{0:T(1024)S(1)}, f32[384,6144]{1,0:T(8,128)}) fusion(bf16[384,64]{0,1:T(8,128)(2,1)} %param.6, bf16[64,6144]{1,0:T(8,128)(2,1)S(1)} %copy-done, bf16[384,6144]{1,0:T(8,128)(2,1)} %param.5), kind=kOutput, calls=%fused_computation.1 | convolution fusion | flops 313780224 | bytes 15015936 | tf_op jit(solution)/shard_map/dot_general | solution.py:46
  9.8 0.4 broadcast_in_dim.7
  10.2 32.3 %all_to_all.25 = f32[32,1,6144]{2,1,0:T(1,128)S(1)} all-to-all(f32[32,1,6144]{2,1,0:T(1,128)S(1)} %broadcast_in_dim.7), channel_id=1, replica_groups=mesh['rows_0'=8,'rows_1'=4,'cols_0'=4,'cols_1'=2] {'rows_0','rows_1'}, dimensions={0} | all-to-all | bytes 1572864 | tf_op jit(solution)/shard_map/all_to_all | solution.py:18
  42.5 0.5 reduce_sum.19
  43.0 6.8 %divide_convert_fusion = bf16[384,6144]{1,0:T(8,128)(2,1)} fusion(f32[384,6144]{1,0:T(8,128)} %get-tuple-element.4, f32[6144]{0:T(1024)S(1)} %sqrt.7), kind=kLoop, calls=%fused_computation | loop fusion | flops 4718592 | bytes 14180352 | tf_op jit(solution)/shard_map/convert_element_type | solution.py:51
  49.8 0.0 copy-start.3
  49.8 0.0 copy-start.1
  49.8 0.0 copy-start.2
  49.8 6.7 %copy.20 = bf16[384,6144]{0,1:T(8,128)(2,1)} copy(bf16[384,6144]{1,0:T(8,128)(2,1)} %divide_convert_fusion) | data formatting | bytes 9437184 | tf_op jit(solution)/shard_map/convert_element_type | solution.py:51
  56.6 5.5 %all-to-all-start.1 = ((bf16[384,32,192]{0,2,1:T(8,128)(2,1)}), bf16[384,32,192]{0,2,1:T(8,128)(2,1)}, u32[]{:S(2)}, u32[]{:S(2)}) async-start(bf16[384,32,192]{0,2,1:T(8,128)(2,1)} %bitcast.11), calls=%async_computation.1 | async-start | bytes 9437184 | tf_op jit(solution)/shard_map/all_to_all | solution.py:52
  62.1 0.0 copy-done.3
  62.1 0.6 dynamic-slice
  63.4 0.0 copy-done.1
  63.4 0.0 copy-done.2
  63.4 0.2 dynamic-update-slice
  63.7 11.0 %all-reduce = bf16[192]{0:T(256)(128)(2,1)S(1)} all-reduce(bf16[192]{0:T(256)(128)(2,1)S(1)} %dynamic-update-slice), channel_id=2, replica_groups=mesh['rows_0'=8,'rows_1'=4,'cols_0'=4,'cols_1'=2] {'rows_1'}, use_global_device_ids=true, to_apply=%add | all-reduce | flops 192 | bytes 768
  74.6 0.1 reshape.24
  74.7 96.1 %all-gather.1 = bf16[8,4,48]{2,1,0:T(4,128)(2,1)S(1)} all-gather(bf16[1,4,48]{2,1,0:T(4,128)(2,1)S(1)} %reshape.24), channel_id=1, replica_groups=mesh['rows_0'=8,'rows_1'=4,'cols_0'=4,'cols_1'=2] {'rows_0'}, dimensions={0}, use_global_device_ids=true | all-gather | bytes 3456 | tf_op jit(solution)/shard_map/all_gather | solution.py:34
  170.8 9.4 %all_gather.14 = bf16[128,48]{1,0:T(8,128)(2,1)S(1)} all-gather(bf16[32,48]{1,0:T(8,128)(2,1)S(1)} %bitcast.14), channel_id=1, replica_groups=mesh['rows_0'=8,'rows_1'=4,'cols_0'=4,'cols_1'=2] {'cols_0'}, dimensions={0}, use_global_device_ids=true | all-gather | bytes 15360 | tf_op jit(solution)/shard_map/all_gather | solution.py:34
  180.2 10.2 %all_gather.15 = bf16[256,48]{1,0:T(8,128)(2,1)S(1)} all-gather(bf16[128,48]{1,0:T(8,128)(2,1)S(1)} %all_gather.14), channel_id=1, replica_groups=mesh['rows_0'=8,'rows_1'=4,'cols_0'=4,'cols_1'=2] {'cols_1'}, dimensions={0}, use_global_device_ids=true | all-gather | bytes 36864 | tf_op jit(solution)/shard_map/all_gather | solution.py:34
  190.5 0.1 copy.22
  190.5 0.7 reshape_reshape.3
  191.3 0.6 dynamic_slice.3
  191.9 0.0 all-to-all-done.1
  191.9 5.3 %copy.24 = bf16[32,24,8,384]{3,2,0,1:T(8,128)(2,1)} copy(bf16[32,24,8,384]{3,2,1,0:T(8,128)(2,1)} %bitcast.7) | data formatting | bytes 9437184 | tf_op jit(solution)/shard_map/all_to_all | solution.py:52
  (3 shorter events, 0.0 us)
Async XLA Ops:
  0.6 1.1 copy-start
  49.8 12.3 %copy-start.3 = (u32[256]{0:T(256)S(1)}, u32[256]{0:T(256)}, u32[]{:S(2)}) copy-start(u32[256]{0:T(256)} %constant.26) | copy-start | bytes 3076
  49.8 13.5 %copy-start.1 = (f32[48]{0:T(128)S(1)}, f32[48]{0:T(128)}, u32[]{:S(2)}) copy-start(f32[48]{0:T(128)} %param.8) | copy-start | bytes 580
  49.8 13.5 %copy-start.2 = (f32[48]{0:T(128)S(1)}, f32[48]{0:T(128)}, u32[]{:S(2)}) copy-start(f32[48]{0:T(128)} %param.9) | copy-start | bytes 580
  56.6 135.3 %all-to-all-start.1 = ((bf16[384,32,192]{0,2,1:T(8,128)(2,1)}), bf16[384,32,192]{0,2,1:T(8,128)(2,1)}, u32[]{:S(2)}, u32[]{:S(2)}) async-start(bf16[384,32,192]{0,2,1:T(8,128)(2,1)} %bitcast.11), calls=%async_computation.1 | async-start | bytes 9437184 | tf_op jit(solution)/shard_map/all_to_all | solution.py:52
where the time goes:
time: 199 us; the launch traced here: 197 us
  blocking collectives  159 us (80%)
  local copies, waits for them, and re-layouts  16 us (8%)
  matrix products  8.02 us (4%)
  other arithmetic  7.29 us (4%)
  starting transfers between devices  5.51 us (3%)
    all_gather x3, blocking collectives, stacked_from(): pieces = lax.all_gather(pieces, axes[k], axis=0, tiled=True)  116 us
    all_to_all x1, blocking collectives, copy_for_each(): return lax.all_to_all(copies, axis, split_axis=0, concat_axis=0, tiled=True)  32.3 us
    unnamed x1, blocking collectives  11 us
    dot_general x1, matrix products, per_device(): jnp.dot(low_up, high_up, preferred_element_type=jnp.float32)  8.02 us
    convert_element_type x1, other arithmetic, per_device(): narrow_up = (fresh_up / scale_up).astype(jnp.bfloat16)  6.83 us
    convert_element_type x1, local copies, waits for them, and re-layouts, per_device(): narrow_up = (fresh_up / scale_up).astype(jnp.bfloat16)  6.75 us
    all_to_all x1, starting transfers between devices, per_device(): lax.all_to_all(narrow_up, ROWS, split_axis=1, concat_axis=0, tiled=True)  5.51 us
    all_to_all x1, local copies, waits for them, and re-layouts, per_device(): lax.all_to_all(narrow_up, ROWS, split_axis=1, concat_axis=0, tiled=True)  5.32 us
  transfers between devices with their start and end apart: 1, of which 0 were waited for; matrix products, arithmetic and copies ran while one was open for 1% of the time, Pallas kernels for 0%

commit v1 on v0

v1 whole, which is shorter than its diff:
```python
import functools

import jax
import jax.numpy as jnp
from jax import lax
from jax.experimental import pallas as pl
from jax.experimental.pallas import tpu as pltpu
from jax.sharding import Mesh
from jax.sharding import PartitionSpec as P

MESH = pl.DeviceIdType.MESH
Z, Y, X, C = 8, 4, 4, 2
PLANE = Z * Y
D_MODEL, RANK = 12288, 64
ROWS = D_MODEL // PLANE
COLS = 6144
MINE = COLS // PLANE
PIECE = D_MODEL // (PLANE * X * C)
STRIDE = 13

mix_rate = 0.5


def comm_kernel(
    w_hbm, low_hbm, high_hbm, train_hbm, step_hbm,
    fresh_ref, inv_ref, scale_ref, norm_ref,
    wbuf, stage, recv, lowbuf, nbuf, hpair, ht, acc, low_ref, nt_ref, ns_ref,
    wsem, isem, ssend, srecv, nsend, nrecv, psend, precv,
):
    z, y = lax.axis_index("z"), lax.axis_index("y")
    x, c = lax.axis_index("x"), lax.axis_index("c")
    row = z * Y + y

    def plane_device(dz, dy):
        return {"z": lax.rem(z + dz, Z), "y": lax.rem(y + dy, Y)}

    def side_device(k):
        other = lax.rem(x * C + c + k, X * C)
        return {"x": other // C, "c": lax.rem(other, C)}

    def weight_copy(p):
        return pltpu.make_async_copy(
            w_hbm.at[:, pl.ds(pl.multiple_of(p * 2 * MINE, 128), 2 * MINE)], wbuf.at[p], wsem.at[p]
        )

    for p in range(PLANE // 2):
        weight_copy(p).start()
    pair = high_hbm.at[:, pl.ds(pl.multiple_of((row // 2) * 2 * MINE, 128), 2 * MINE)]
    small = [
        pltpu.make_async_copy(ref, to, isem.at[k])
        for k, (ref, to) in enumerate(((train_hbm, nt_ref), (step_hbm, ns_ref), (low_hbm, low_ref), (pair, hpair)))
    ]
    for copy in small:
        copy.start()

    barrier = pltpu.get_barrier_semaphore()
    for d in range(1, PLANE):
        pl.semaphore_signal(barrier, inc=1, device_id=plane_device(d // Y, d % Y), device_id_type=MESH)
    for k in range(1, X * C):
        pl.semaphore_signal(barrier, inc=1, device_id=side_device(k), device_id_type=MESH)

    me = x * C + c
    for copy in small:
        copy.wait()
    gain = (nt_ref[...] + ns_ref[...]).astype(jnp.bfloat16).astype(jnp.float32)
    spot = me * PIECE + lax.broadcasted_iota(jnp.int32, (16, PIECE), 1)
    in_row = spot // 128 == lax.broadcasted_iota(jnp.int32, (16, PIECE), 0)
    left = jnp.where(in_row, jnp.broadcast_to(gain, (16, PIECE)), 0.0).astype(jnp.bfloat16)
    lane = lax.rem(me * PIECE + lax.broadcasted_iota(jnp.int32, (PIECE, 128), 0), 128)
    right = jnp.where(lane == lax.broadcasted_iota(jnp.int32, (PIECE, 128), 1), 1.0, 0.0).astype(jnp.bfloat16)
    nbuf[me] = jnp.dot(left, right, preferred_element_type=jnp.float32).astype(jnp.bfloat16)

    lowbuf[x, z, y, :, 0:ROWS] = low_ref[pl.ds(pl.multiple_of(x * 16, 16), 16), :]

    wide = jnp.concatenate([hpair[...].astype(jnp.float32), jnp.zeros((RANK, 2 * MINE), jnp.float32)], axis=0)
    ht[...] = wide.T
    mine = pl.ds(pl.multiple_of(lax.rem(row, 2) * MINE, 8), MINE)
    high_t = ht[mine, :][:, 0:RANK].astype(jnp.bfloat16)

    @pl.loop(0, PLANE // 2)
    def _(p):
        weight_copy(p).wait()
        turned = wbuf[p].T
        stage[2 * p] = turned[0:MINE]
        stage[2 * p + 1] = turned[MINE : 2 * MINE]

    pl.semaphore_wait(barrier, PLANE - 1 + X * C - 1)

    def block_copy(d):
        dz, dy = d // Y, lax.rem(d, Y)
        to_z, to_y = lax.rem(z + dz, Z), lax.rem(y + dy, Y)
        return pltpu.make_async_remote_copy(
            src_ref=stage.at[to_z * Y + to_y], dst_ref=recv.at[d], send_sem=ssend.at[d], recv_sem=srecv.at[d],
            device_id={"z": to_z, "y": to_y}, device_id_type=MESH,
        )

    def send_blocks(first, last):
        @pl.loop(first, last)
        def _(i):
            block_copy(lax.rem(i * STRIDE, PLANE)).start()

    send_blocks(1, 5)

    def gain_copy(k):
        return pltpu.make_async_remote_copy(
            src_ref=nbuf.at[me], dst_ref=nbuf.at[me], send_sem=nsend.at[k], recv_sem=nrecv.at[k],
            device_id=side_device(k), device_id_type=MESH,
        )

    for k in range(1, X * C):
        gain_copy(k).start()
    for k in range(1, X * C):
        gain_copy(k).wait()
    gains = nbuf[0].astype(jnp.float32)
    for k in range(1, X * C):
        gains = gains + nbuf[k].astype(jnp.float32)
    lowbuf[x, z, y, :, ROWS : ROWS + 128] = gains.astype(jnp.bfloat16)

    def hop_copy(ref, slot, device):
        return pltpu.make_async_remote_copy(
            src_ref=ref, dst_ref=ref, send_sem=psend.at[slot], recv_sem=precv.at[slot],
            device_id=device, device_id_type=MESH,
        )

    along_z = [hop_copy(lowbuf.at[x, z, y], k - 1, {"z": lax.rem(z + k, Z)}) for k in range(1, Z)]
    along_y = [hop_copy(lowbuf.at[x, :, y], Z - 2 + k, {"y": lax.rem(y + k, Y)}) for k in range(1, Y)]
    along_x = [hop_copy(lowbuf.at[x], Z + Y - 3 + k, {"x": lax.rem(x + k, X)}) for k in range(1, X)]
    for copy in along_z:
        copy.start()
    send_blocks(5, 11)
    for copy in along_z:
        copy.wait()
    for copy in along_y:
        copy.start()
    send_blocks(11, 18)
    for copy in along_y:
        copy.wait()
    for copy in along_x:
        copy.start()
    send_blocks(18, PLANE)
    for copy in along_x:
        copy.wait()

    acc[...] = jnp.zeros_like(acc)

    def add_block(block, from_z, from_y):
        low = jnp.concatenate([lowbuf[k, from_z, from_y, :, 0:ROWS] for k in range(X)], axis=0)
        fresh = block.astype(jnp.float32) + mix_rate * jnp.dot(high_t, low, preferred_element_type=jnp.float32)
        from_row = from_z * Y + from_y
        fresh_ref[:, pl.ds(pl.multiple_of(from_row * ROWS, 128), ROWS)] = fresh
        square = fresh * fresh
        acc[...] += square[:, 0:128] + square[:, 128:256] + square[:, 256:384]

    add_block(stage[row], z, y)

    @pl.loop(0, PLANE)
    def _(r):
        norm_ref[pl.ds(r * 3, 3), :] = lowbuf[0, r // Y, lax.rem(r, Y), 0:16, ROWS : ROWS + 128].astype(jnp.float32)[0:3]

    @pl.loop(1, PLANE)
    def _(i):
        d = lax.rem(i * STRIDE, PLANE)
        block_copy(d).wait()
        add_block(recv[d], lax.rem(z - d // Y + Z, Z), lax.rem(y - lax.rem(d, Y) + Y, Y))

    scale = jnp.broadcast_to(jnp.sqrt(jnp.sum(acc[...], axis=1, keepdims=True)), (MINE, 128))
    inv_ref[...] = 1.0 / scale
    scale_ref[...] = jnp.concatenate([scale, jnp.zeros((64, 128), jnp.float32)], axis=0).T[0:8]


def scale_kernel(fresh_ref, inv_ref, serve_ref):
    width = serve_ref.shape[1]
    at = pl.program_id(0) * width
    inv = inv_ref[...]
    for k in range(width // 128):
        part = fresh_ref[:, pl.ds(pl.multiple_of(at + k * 128, 128), 128)]
        serve_ref[:, k * 128 : (k + 1) * 128] = (part * inv).astype(jnp.bfloat16)


def per_device(weight_up, low_up, high_up, norm_train, norm_step):
    vmem = pl.BlockSpec(memory_space=pltpu.VMEM)
    hbm = pl.BlockSpec(memory_space=pltpu.HBM)
    bf16, f32 = jnp.bfloat16, jnp.float32
    dma = pltpu.SemaphoreType.DMA
    operands = weight_up, low_up.T, high_up, norm_train.reshape(1, PIECE), norm_step.reshape(1, PIECE)
    fresh, inv, scale, norm = pl.pallas_call(
        comm_kernel,
        out_shape=(
            pltpu.VMEM((MINE, D_MODEL), f32),
            pltpu.VMEM((MINE, 128), f32),
            jax.ShapeDtypeStruct((8, 256), f32),
            jax.ShapeDtypeStruct((D_MODEL // 128, 128), f32),
        ),
        in_specs=[hbm] * 5,
        out_specs=(vmem, vmem, vmem, vmem),
        scratch_shapes=[
            pltpu.VMEM((PLANE // 2, ROWS, 2 * MINE), bf16),
            pltpu.VMEM((PLANE, MINE, ROWS), bf16),
            pltpu.VMEM((PLANE, MINE, ROWS), bf16),
            pltpu.VMEM((X, Z, Y, 16, ROWS + 128), bf16),
            pltpu.VMEM((X * C, 16, 128), bf16),
            pltpu.VMEM((RANK, 2 * MINE), bf16),
            pltpu.VMEM((2 * MINE, 128), f32),
            pltpu.VMEM((MINE, 128), f32),
            pltpu.VMEM((RANK, ROWS), bf16),
            pltpu.VMEM((1, PIECE), f32),
            pltpu.VMEM((1, PIECE), f32),
            dma((PLANE // 2,)), dma((4,)), dma((PLANE,)), dma((PLANE,)),
            dma((X * C,)), dma((X * C,)), dma((Z + Y + X - 3,)), dma((Z + Y + X - 3,)),
        ],
        compiler_params=pltpu.CompilerParams(
            collective_id=0, has_side_effects=True, vmem_limit_bytes=40 * 2**20
        ),
        name="exchange",
    )(*(pltpu.with_memory_space_constraint(a, pltpu.HBM) for a in operands))
    steps = 8
    serve_t = pl.pallas_call(
        scale_kernel,
        grid=(steps,),
        out_shape=jax.ShapeDtypeStruct((MINE, D_MODEL), bf16),
        in_specs=[vmem, vmem],
        out_specs=pl.BlockSpec((MINE, D_MODEL // steps), lambda i: (0, i)),
        compiler_params=pltpu.CompilerParams(vmem_limit_bytes=16 * 2**20),
        name="rescale",
    )(fresh, inv)
    return serve_t.T, scale[0, :MINE], norm.reshape(-1).astype(bf16)


def solution(mesh):
    split = Mesh(mesh.devices.reshape(Z, Y, X, C), ("z", "y", "x", "c"))
    rows, cols = ("z", "y"), ("x", "c")
    in_specs = (P(rows, cols), P(rows, None), P(None, cols), P(rows + cols), P(rows + cols))
    out_specs = (P(None, cols + rows), P(cols + rows), P())
    return jax.shard_map(per_device, mesh=split, in_specs=in_specs, out_specs=out_specs, check_vma=False)
```

time: 199 us -> 126 us (0.63)
  blocking collectives: 159 us -> 0 us
  Pallas kernels: 0 us -> 124 us
  local copies, waits for them, and re-layouts: 16 us -> 0.56 us
  matrix products: 8.02 us -> 0 us
  other arithmetic: 7.29 us -> 0.61 us
  starting transfers between devices: 5.51 us -> 0 us
    pallas_call x0 -> x2, Pallas kernels: none -> 124 us  [the longest x1 120 us: per_device(): pl.pallas_call(comm_kernel, out_shape=(pltpu.VMEM((MINE, D_MODEL), f32),...]
    all_gather x3 -> x0, blocking collectives: 116 us -> none  [stacked_from(): pieces = lax.all_gather(pieces, axes[k], axis=0, tiled=True)]
    all_to_all x1 -> x0, blocking collectives: 32.3 us -> none  [copy_for_each(): return lax.all_to_all(copies, axis, split_axis=0, concat_axis=0, tiled=True)]
    unnamed x1 -> x0, blocking collectives: 11 us -> none
    dot_general x1 -> x0, matrix products: 8.02 us -> none  [per_device(): jnp.dot(low_up, high_up, preferred_element_type=jnp.float32)]
    convert_element_type x1 -> x0, local copies, waits for them, and re-layouts: 6.75 us -> none  [per_device(): narrow_up = (fresh_up / scale_up).astype(jnp.bfloat16)]
    convert_element_type x2 -> x1, other arithmetic: 6.84 us -> 0.61 us  [per_device(): return (serve_t.T, scale[0, :MINE], norm.reshape(-1).astype(bf16))]
    all_to_all x1 -> x0, starting transfers between devices: 5.51 us -> none  [per_device(): lax.all_to_all(narrow_up, ROWS, split_axis=1, concat_axis=0, tiled=True)]
  transfers between devices with their start and end apart: 1 -> 0, of which waited for: 0 -> 0; matrix products, arithmetic and copies ran while one was open for 1% -> 0% of each run, Pallas kernels for 0% -> 0%
where the time goes in v1:
time: 126 us
  Pallas kernels  124 us (98%)
    pallas_call x1, Pallas kernels, per_device(): pl.pallas_call(comm_kernel, out_shape=(pltpu.VMEM((MINE, D_MODEL), f32),...  120 us
    pallas_call x1, Pallas kernels, per_device(): pl.pallas_call(scale_kernel, grid=(steps,), out_shape=jax.ShapeDtypeStruc...  4.14 us

profile of v1, /device:TPU:9, one launch (start us, length us, event | category | flops | bytes accessed | tf_op | source)
XLA Modules:
  0.0 126.0 jit_solution(12850771458331324940)
XLA Ops:
  0.6 120.1 %exchange.1 = (f32[192,12288]{1,0:T(8,128)S(1)}, f32[192,128]{1,0:T(8,128)S(1)}, f32[8,256]{1,0:T(8,128)S(1)}, f32[96,128]{1,0:T(8,128)S(1)}) custom-call(bf16[384,6144]{1,0:T(8,128)(2,1)} %w_hbm.1, bf16[64,384]{1,0:T(8,128)(2,1)} %bitcast.8, bf16[64,6144]{1,0:T(8,128)(2,1)} %high_hbm.1, f32[1,48]{1,0:T(1,128)} %bitcast.10, f32[1,48]{1,0:T(1,128)} %bitcast.11), custom_call_target="tpu_custom_call" | custom-call | tf_op jit(solution)/shard_map/exchange/pallas_call | solution.py:186
  120.7 4.1 %rescale.1 = bf16[192,12288]{1,0:T(8,128)(2,1)} custom-call(f32[192,12288]{1,0:T(8,128)S(1)} %get-tuple-element.7.fresh_ref, f32[192,128]{1,0:T(8,128)S(1)} %get-tuple-element.8.inv_ref), custom_call_target="tpu_custom_call" | custom-call | tf_op jit(solution)/shard_map/rescale/pallas_call | solution.py:217
  124.9 0.6 slice.3
  125.4 0.6 convert_bitcast_fusion

commit v2 on v1

v2 whole, which is shorter than its diff:
```python
import functools

import jax
import jax.numpy as jnp
from jax import lax
from jax.experimental import pallas as pl
from jax.experimental.pallas import tpu as pltpu
from jax.sharding import Mesh
from jax.sharding import PartitionSpec as P

MESH = pl.DeviceIdType.MESH
Z, Y, X, C = 8, 4, 4, 2
PLANE = Z * Y
D_MODEL, RANK = 12288, 64
ROWS = D_MODEL // PLANE
COLS = 6144
MINE = COLS // PLANE
PIECE = D_MODEL // (PLANE * X * C)
STEPS = PLANE // 2
ORDER, START = 7, 7
AFTER_Z, AFTER_Y = 2, 2
WRITES = 2
HEAD = 4

mix_rate = 0.5


def comm_kernel(
    w_hbm, low_hbm, high_hbm, train_hbm, step_hbm,
    fresh_ref, inv_ref, scale_ref, norm_ref,
    wbuf, stage, recv, lowbuf, nbuf, hpair, ht, acc, norms, low_ref, nt_ref, ns_ref,
    wsem, isem, ssend, srecv, nsend, nrecv, psend, precv,
):
    z, y = lax.axis_index("z"), lax.axis_index("y")
    x, c = lax.axis_index("x"), lax.axis_index("c")
    row = z * Y + y
    me = x * C + c

    def step(s):
        t = lax.rem(s * ORDER + START, STEPS)
        return t // 2, lax.rem(t, 2)

    def partner(dz, q, j):
        return lax.rem(z + dz, Z), 2 * lax.rem(y // 2 + q, 2) + lax.rem(y + j, 2)

    def side_device(k):
        other = lax.rem(me + k, X * C)
        return {"x": other // C, "c": lax.rem(other, C)}

    def pair_of(s):
        dz, q = step(s)
        to_z, to_y = partner(dz, q, 0)
        return to_z * (Y // 2) + to_y // 2

    def weight_copy(s):
        return pltpu.make_async_copy(
            w_hbm.at[:, pl.ds(pl.multiple_of(pair_of(s) * 2 * MINE, 128), 2 * MINE)], wbuf.at[s], wsem.at[s]
        )

    for s in range(2):
        weight_copy(s).start()

    barrier = pltpu.get_barrier_semaphore()
    for t in range(1, PLANE):
        to_z, to_y = partner(t // Y, t % Y // 2, t % 2)
        pl.semaphore_signal(barrier, inc=1, device_id={"z": to_z, "y": to_y}, device_id_type=MESH)
    for k in range(1, X * C):
        pl.semaphore_signal(barrier, inc=1, device_id=side_device(k), device_id_type=MESH)

    for s in range(2, HEAD):
        weight_copy(s).start()
    pair = high_hbm.at[:, pl.ds(pl.multiple_of((row // 2) * 2 * MINE, 128), 2 * MINE)]
    small = [
        pltpu.make_async_copy(ref, to, isem.at[k])
        for k, (ref, to) in enumerate(((train_hbm, nt_ref), (step_hbm, ns_ref), (low_hbm, low_ref), (pair, hpair)))
    ]
    for copy in small:
        copy.start()
    for s in range(HEAD, STEPS):
        weight_copy(s).start()

    def turn(s):
        weight_copy(s).wait()
        turned = wbuf[s].T
        stage[2 * s] = turned[0:MINE]
        stage[2 * s + 1] = turned[MINE : 2 * MINE]

    def block_copy(s, j):
        dz, q = step(s)
        to_z, to_y = partner(dz, q, j)
        slot = dz * Y + 2 * q + j
        return pltpu.make_async_remote_copy(
            src_ref=stage.at[2 * s + lax.rem(to_y, 2)], dst_ref=recv.at[slot],
            send_sem=ssend.at[slot], recv_sem=srecv.at[slot],
            device_id={"z": to_z, "y": to_y}, device_id_type=MESH,
        )

    def send(s):
        dz, q = step(s)

        @pl.when(dz + q > 0)
        def _():
            block_copy(s, 0).start()

        block_copy(s, 1).start()

    @pl.loop(0, HEAD)
    def _(s):
        turn(s)

    for copy in small:
        copy.wait()
    gain = (nt_ref[...] + ns_ref[...]).astype(jnp.bfloat16).astype(jnp.float32)
    spot = me * PIECE + lax.broadcasted_iota(jnp.int32, (16, PIECE), 1)
    in_row = spot // 128 == lax.broadcasted_iota(jnp.int32, (16, PIECE), 0)
    left = jnp.where(in_row, jnp.broadcast_to(gain, (16, PIECE)), 0.0).astype(jnp.bfloat16)
    lane = lax.rem(me * PIECE + lax.broadcasted_iota(jnp.int32, (PIECE, 128), 0), 128)
    right = jnp.where(lane == lax.broadcasted_iota(jnp.int32, (PIECE, 128), 1), 1.0, 0.0).astype(jnp.bfloat16)
    nbuf[me] = jnp.dot(left, right, preferred_element_type=jnp.float32).astype(jnp.bfloat16)

    ranks = pl.ds(pl.multiple_of(x * 16, 16), 16)

    @pl.when(c == 0)
    def _():
        lowbuf[0, x, z, y] = low_ref[ranks, 0:256]

    @pl.when(c == 1)
    def _():
        lowbuf[1, x, z, y, :, 0:128] = low_ref[ranks, 256:384]

    pl.semaphore_wait(barrier, PLANE - 1 + X * C - 1)

    def gain_copy(k):
        return pltpu.make_async_remote_copy(
            src_ref=nbuf.at[me], dst_ref=nbuf.at[me], send_sem=nsend.at[k], recv_sem=nrecv.at[k],
            device_id=side_device(k), device_id_type=MESH,
        )

    for s in range(HEAD - 1):
        send(s)
    for k in range(1, X * C):
        gain_copy(k).start()

    def turn_and_send(first, last):
        @pl.loop(first, last)
        def _(s):
            turn(s)
            send(s - 1)

    turn_and_send(HEAD, HEAD + 3)
    for k in range(1, X * C):
        gain_copy(k).wait()
    gains = nbuf[0].astype(jnp.float32)
    for k in range(1, X * C):
        gains = gains + nbuf[k].astype(jnp.float32)

    @pl.when(c == 1)
    def _():
        lowbuf[1, x, z, y, :, 128:256] = gains.astype(jnp.bfloat16)

    def hop_copy(ref, slot, device):
        return pltpu.make_async_remote_copy(
            src_ref=ref, dst_ref=ref, send_sem=psend.at[slot], recv_sem=precv.at[slot],
            device_id=device, device_id_type=MESH,
        )

    along_z = [hop_copy(lowbuf.at[c, x, z, y], k - 1, {"z": lax.rem(z + k, Z)}) for k in range(1, Z)]
    along_y = [hop_copy(lowbuf.at[c, x, :, y], Z - 2 + k, {"y": lax.rem(y + k, Y)}) for k in range(1, Y)]
    aside = [hop_copy(lowbuf.at[c, x], Z + Y - 3 + k, side_device(k)) for k in range(1, X * C)]
    turn_and_send(HEAD + 3, HEAD + 4)
    for copy in along_z:
        copy.start()
    turn_and_send(HEAD + 4, STEPS - AFTER_Z - AFTER_Y)

    @pl.loop(STEPS - AFTER_Z - AFTER_Y, STEPS)
    def _(s):
        turn(s)

    for copy in along_z:
        copy.wait()
    for copy in along_y:
        copy.start()
    for s in range(STEPS - AFTER_Z - AFTER_Y - 1, STEPS - AFTER_Y - 1):
        send(s)
    for copy in along_y:
        copy.wait()
    for copy in aside:
        copy.start()
    for s in range(STEPS - AFTER_Y - 1, STEPS):
        send(s)

    wide = jnp.concatenate([hpair[...].astype(jnp.float32), jnp.zeros((RANK, 2 * MINE), jnp.float32)], axis=0)
    ht[...] = wide.T
    mine = pl.ds(pl.multiple_of(lax.rem(row, 2) * MINE, 8), MINE)
    high_t = ht[mine, :][:, 0:RANK].astype(jnp.bfloat16)

    for copy in aside:
        copy.wait()

    acc[...] = jnp.zeros_like(acc)

    def add_block(block, from_z, from_y):
        low = jnp.concatenate(
            [
                jnp.concatenate([lowbuf[0, k, from_z, from_y], lowbuf[1, k, from_z, from_y, :, 0:128]], axis=1)
                for k in range(X)
            ],
            axis=0,
        )
        fresh = block.astype(jnp.float32) + mix_rate * jnp.dot(high_t, low, preferred_element_type=jnp.float32)
        from_row = from_z * Y + from_y
        fresh_ref[:, pl.ds(pl.multiple_of(from_row * ROWS, 128), ROWS)] = fresh
        square = fresh * fresh
        acc[...] += square[:, 0:128] + square[:, 128:256] + square[:, 256:384]

    @pl.loop(0, PLANE)
    def _(r):
        norms[pl.ds(r * 3, 3), :] = lowbuf[1, 0, r // Y, lax.rem(r, Y), :, 128:256].astype(jnp.float32)[0:3]

    norm_ref[...] = norms[...].astype(jnp.bfloat16)

    @pl.loop(0, STEPS)
    def _(s):
        dz, q = step(s)

        @pl.loop(0, 2)
        def _(j):
            away = dz + q + j > 0
            from_z = lax.rem(z + Z - dz, Z)
            from_y = partner(dz, q, j)[1]

            @pl.when(away)
            def _():
                block_copy(s, j).wait()
                add_block(recv[dz * Y + 2 * q + j], from_z, from_y)

            @pl.when(jnp.logical_not(away))
            def _():
                add_block(stage[2 * s + lax.rem(y, 2)], z, y)

    scale = jnp.broadcast_to(jnp.sqrt(jnp.sum(acc[...], axis=1, keepdims=True)), (MINE, 128))
    inv_ref[...] = 1.0 / scale
    scale_ref[...] = jnp.concatenate([scale, jnp.zeros((64, 128), jnp.float32)], axis=0).T[0:8]


def scale_kernel(fresh_ref, inv_ref, scale_ref, norm_ref, serve_ref, scale_out, norm_out):
    width = serve_ref.shape[1]
    at = pl.program_id(0) * width
    inv = inv_ref[...]
    for k in range(width // 128):
        part = fresh_ref[:, pl.ds(pl.multiple_of(at + k * 128, 128), 128)]
        serve_ref[:, k * 128 : (k + 1) * 128] = (part * inv).astype(jnp.bfloat16)

    @pl.when(pl.program_id(0) == 0)
    def _():
        scale_out[...] = scale_ref[0:1, 0:MINE]
        norm_out[...] = norm_ref[...]


def per_device(weight_up, low_up, high_up, norm_train, norm_step):
    vmem = pl.BlockSpec(memory_space=pltpu.VMEM)
    hbm = pl.BlockSpec(memory_space=pltpu.HBM)
    bf16, f32 = jnp.bfloat16, jnp.float32
    dma = pltpu.SemaphoreType.DMA
    operands = weight_up, low_up.T, high_up, norm_train.reshape(1, PIECE), norm_step.reshape(1, PIECE)
    hops = Z + Y + X * C - 3
    found = pl.pallas_call(
        comm_kernel,
        out_shape=(
            pltpu.VMEM((MINE, D_MODEL), f32),
            pltpu.VMEM((MINE, 128), f32),
            pltpu.VMEM((8, 256), f32),
            pltpu.VMEM((D_MODEL // 128, 128), bf16),
        ),
        in_specs=[hbm] * 5,
        out_specs=(vmem, vmem, vmem, vmem),
        scratch_shapes=[
            pltpu.VMEM((STEPS, ROWS, 2 * MINE), bf16),
            pltpu.VMEM((PLANE, MINE, ROWS), bf16),
            pltpu.VMEM((PLANE, MINE, ROWS), bf16),
            pltpu.VMEM((C, X, Z, Y, 16, 256), bf16),
            pltpu.VMEM((X * C, 16, 128), bf16),
            pltpu.VMEM((RANK, 2 * MINE), bf16),
            pltpu.VMEM((2 * MINE, 128), f32),
            pltpu.VMEM((MINE, 128), f32),
            pltpu.VMEM((D_MODEL // 128, 128), f32),
            pltpu.VMEM((RANK, ROWS), bf16),
            pltpu.VMEM((1, PIECE), f32),
            pltpu.VMEM((1, PIECE), f32),
            dma((STEPS,)), dma((4,)), dma((PLANE,)), dma((PLANE,)),
            dma((X * C,)), dma((X * C,)), dma((hops,)), dma((hops,)),
        ],
        compiler_params=pltpu.CompilerParams(
            collective_id=0, has_side_effects=True, vmem_limit_bytes=40 * 2**20
        ),
        name="exchange",
    )(*(pltpu.with_memory_space_constraint(a, pltpu.HBM) for a in operands))
    serve_t, scale, norm = pl.pallas_call(
        scale_kernel,
        grid=(WRITES,),
        out_shape=(
            jax.ShapeDtypeStruct((MINE, D_MODEL), bf16),
            jax.ShapeDtypeStruct((1, MINE), f32),
            jax.ShapeDtypeStruct((D_MODEL // 128, 128), bf16),
        ),
        in_specs=[vmem] * 4,
        out_specs=(
            pl.BlockSpec((MINE, D_MODEL // WRITES), lambda i: (0, i)),
            pl.BlockSpec((1, MINE), lambda i: (0, 0)),
            pl.BlockSpec((D_MODEL // 128, 128), lambda i: (0, 0)),
        ),
        compiler_params=pltpu.CompilerParams(vmem_limit_bytes=12 * 2**20),
        name="rescale",
    )(*found)
    return serve_t.T, scale.reshape(-1), norm.reshape(-1)


def solution(mesh):
    split = Mesh(mesh.devices.reshape(Z, Y, X, C), ("z", "y", "x", "c"))
    rows, cols = ("z", "y"), ("x", "c")
    in_specs = (P(rows, cols), P(rows, None), P(None, cols), P(rows + cols), P(rows + cols))
    out_specs = (P(None, cols + rows), P(cols + rows), P())
    return jax.shard_map(per_device, mesh=split, in_specs=in_specs, out_specs=out_specs, check_vma=False)
```

time: 126 us -> 122 us (0.968)
  the two profiles are of different devices: /device:TPU:9 before, /device:TPU:34 now
where the time goes in v2:
time: 122 us
  Pallas kernels  121 us (99%)
    pallas_call x1, Pallas kernels, per_device(): pl.pallas_call(comm_kernel, out_shape=(pltpu.VMEM((MINE, D_MODEL), f32),...  118 us
    pallas_call x1, Pallas kernels, per_device(): pl.pallas_call(scale_kernel, grid=(WRITES,), out_shape=(jax.ShapeDtypeStr...  2.9 us

profile of v2, /device:TPU:34, one launch (start us, length us, event | category | flops | bytes accessed | tf_op | source)
XLA Modules:
  0.0 121.7 jit_solution(15433485501189748124)
XLA Ops:
  0.6 118.2 %exchange.1 = (f32[192,12288]{1,0:T(8,128)S(1)}, f32[192,128]{1,0:T(8,128)S(1)}, f32[8,256]{1,0:T(8,128)S(1)}, bf16[96,128]{1,0:T(8,128)(2,1)S(1)}) custom-call(bf16[384,6144]{1,0:T(8,128)(2,1)} %w_hbm.1, bf16[64,384]{1,0:T(8,128)(2,1)} %bitcast.6, bf16[64,6144]{1,0:T(8,128)(2,1)} %high_hbm.1, f32[1,48]{1,0:T(1,128)} %bitcast.7, f32[1,48]{1,0:T(1,128)} %bitcast.8), custom_call_target="tpu_custom_call" | custom-call | tf_op jit(solution)/shard_map/exchange/pallas_call | solution.py:267
  118.8 2.9 %rescale.1 = (bf16[192,12288]{1,0:T(8,128)(2,1)}, f32[1,192]{1,0:T(1,128)}, bf16[96,128]{1,0:T(8,128)(2,1)}) custom-call(f32[192,12288]{1,0:T(8,128)S(1)} %get-tuple-element.10.fresh_ref, f32[192,128]{1,0:T(8,128)S(1)} %get-tuple-element.11.inv_ref, f32[8,256]{1,0:T(8,128)S(1)} %get-tuple-element.12.scale_ref, bf16[96,128]{1,0:T(8,128)(2,1)S(1)} %get-tuple-element.13.norm_ref), custom_call_target="tpu_custom_call" | custom-call | tf_op jit(solution)/shard_map/rescale/pallas_call | solution.py:298

commit v3 on v2

--- a/solution.py
+++ b/solution.py
@@ -17,10 +17,7 @@
 MINE = COLS // PLANE
 PIECE = D_MODEL // (PLANE * X * C)
 STEPS = PLANE // 2
-ORDER, START = 7, 7
-AFTER_Z, AFTER_Y = 2, 2
 WRITES = 2
-HEAD = 4
 
 mix_rate = 0.5
 
@@ -28,8 +25,8 @@
 def comm_kernel(
     w_hbm, low_hbm, high_hbm, train_hbm, step_hbm,
     fresh_ref, inv_ref, scale_ref, norm_ref,
-    wbuf, stage, recv, lowbuf, nbuf, hpair, ht, acc, norms, low_ref, nt_ref, ns_ref,
-    wsem, isem, ssend, srecv, nsend, nrecv, psend, precv,
+    wbuf, stage, recv, relay, lowbuf, nbuf, hpair, ht, acc, norms, low_ref, nt_ref, ns_ref,
+    wsem, isem, zsend, zrecv, ysend, yrecv, nsend, nrecv, psend, precv,
 ):
     z, y = lax.axis_index("z"), lax.axis_index("y")
     x, c = lax.axis_index("x"), lax.axis_index("c")
@@ -37,8 +34,14 @@
     me = x * C + c
 
     def step(s):
-        t = lax.rem(s * ORDER + START, STEPS)
-        return t // 2, lax.rem(t, 2)
+        return away(lax.rem(s, Z)), 1 - s // Z
+
+    def step_of(dz, q):
+        k = lax.rem(dz + Z - 1, Z)
+        return 2 * lax.rem(k, Z // 2) + k // (Z // 2) + (1 - q) * Z
+
+    def away(k):
+        return lax.rem(1 + k // 2 + Z // 2 * lax.rem(k, 2), Z)
 
     def partner(dz, q, j):
         return lax.rem(z + dz, Z), 2 * lax.rem(y // 2 + q, 2) + lax.rem(y + j, 2)
@@ -61,14 +64,13 @@
         weight_copy(s).start()
 
     barrier = pltpu.get_barrier_semaphore()
-    for t in range(1, PLANE):
-        to_z, to_y = partner(t // Y, t % Y // 2, t % 2)
-        pl.semaphore_signal(barrier, inc=1, device_id={"z": to_z, "y": to_y}, device_id_type=MESH)
+    for k in range(1, Z):
+        pl.semaphore_signal(barrier, inc=1, device_id={"z": lax.rem(z + k, Z)}, device_id_type=MESH)
+    for k in range(1, Y):
+        pl.semaphore_signal(barrier, inc=1, device_id={"y": lax.rem(y + k, Y)}, device_id_type=MESH)
     for k in range(1, X * C):
         pl.semaphore_signal(barrier, inc=1, device_id=side_device(k), device_id_type=MESH)
 
-    for s in range(2, HEAD):
-        weight_copy(s).start()
     pair = high_hbm.at[:, pl.ds(pl.multiple_of((row // 2) * 2 * MINE, 128), 2 * MINE)]
     small = [
         pltpu.make_async_copy(ref, to, isem.at[k])
@@ -76,7 +78,7 @@
     ]
     for copy in small:
         copy.start()
-    for s in range(HEAD, STEPS):
+    for s in range(2, STEPS):
         weight_copy(s).start()
 
     def turn(s):
@@ -85,28 +87,37 @@
         stage[2 * s] = turned[0:MINE]
         stage[2 * s + 1] = turned[MINE : 2 * MINE]
 
-    def block_copy(s, j):
-        dz, q = step(s)
+    def copy_z(dz, e, into):
+        q, j = e // 2, lax.rem(e, 2)
         to_z, to_y = partner(dz, q, j)
-        slot = dz * Y + 2 * q + j
+        slot = dz * Y + e
         return pltpu.make_async_remote_copy(
-            src_ref=stage.at[2 * s + lax.rem(to_y, 2)], dst_ref=recv.at[slot],
-            send_sem=ssend.at[slot], recv_sem=srecv.at[slot],
-            device_id={"z": to_z, "y": to_y}, device_id_type=MESH,
-        )
-
-    def send(s):
-        dz, q = step(s)
-
-        @pl.when(dz + q > 0)
-        def _():
-            block_copy(s, 0).start()
-
-        block_copy(s, 1).start()
-
-    @pl.loop(0, HEAD)
-    def _(s):
-        turn(s)
+            src_ref=stage.at[2 * step_of(dz, q) + lax.rem(to_y, 2)], dst_ref=into.at[slot],
+            send_sem=zsend.at[slot], recv_sem=zrecv.at[slot], device_id={"z": to_z}, device_id_type=MESH,
+        )
+
+    def copy_y(ref, dz, e):
+        slot = dz * Y + e
+        return pltpu.make_async_remote_copy(
+            src_ref=ref, dst_ref=recv.at[slot], send_sem=ysend.at[slot], recv_sem=yrecv.at[slot],
+            device_id={"y": partner(dz, e // 2, lax.rem(e, 2))[1]}, device_id_type=MESH,
+        )
+
+    def each(first, last, do):
+        @pl.loop(first, last)
+        def _(k):
+            do(k)
+
+    def turn_and_send(first, last, e):
+        @pl.loop(first, last)
+        def _(s):
+            turn(s)
+            copy_z(step(s - 1)[0], e, relay).start()
+
+    turn(0)
+    turn(1)
+    pl.semaphore_wait(barrier, Z - 1 + Y - 1 + X * C - 1)
+    copy_z(1, 2, relay).start()
 
     for copy in small:
         copy.wait()
@@ -128,26 +139,15 @@
     def _():
         lowbuf[1, x, z, y, :, 0:128] = low_ref[ranks, 256:384]
 
-    pl.semaphore_wait(barrier, PLANE - 1 + X * C - 1)
-
     def gain_copy(k):
         return pltpu.make_async_remote_copy(
             src_ref=nbuf.at[me], dst_ref=nbuf.at[me], send_sem=nsend.at[k], recv_sem=nrecv.at[k],
             device_id=side_device(k), device_id_type=MESH,
         )
 
-    for s in range(HEAD - 1):
-        send(s)
     for k in range(1, X * C):
         gain_copy(k).start()
-
-    def turn_and_send(first, last):
-        @pl.loop(first, last)
-        def _(s):
-            turn(s)
-            send(s - 1)
-
-    turn_and_send(HEAD, HEAD + 3)
+    turn_and_send(2, Z, 2)
     for k in range(1, X * C):
         gain_copy(k).wait()
     gains = nbuf[0].astype(jnp.float32)
@@ -167,33 +167,37 @@
     along_z = [hop_copy(lowbuf.at[c, x, z, y], k - 1, {"z": lax.rem(z + k, Z)}) for k in range(1, Z)]
     along_y = [hop_copy(lowbuf.at[c, x, :, y], Z - 2 + k, {"y": lax.rem(y + k, Y)}) for k in range(1, Y)]
     aside = [hop_copy(lowbuf.at[c, x], Z + Y - 3 + k, side_device(k)) for k in range(1, X * C)]
-    turn_and_send(HEAD + 3, HEAD + 4)
     for copy in along_z:
         copy.start()
-    turn_and_send(HEAD + 4, STEPS - AFTER_Z - AFTER_Y)
-
-    @pl.loop(STEPS - AFTER_Z - AFTER_Y, STEPS)
-    def _(s):
-        turn(s)
-
-    for copy in along_z:
-        copy.wait()
-    for copy in along_y:
-        copy.start()
-    for s in range(STEPS - AFTER_Z - AFTER_Y - 1, STEPS - AFTER_Y - 1):
-        send(s)
-    for copy in along_y:
-        copy.wait()
-    for copy in aside:
-        copy.start()
-    for s in range(STEPS - AFTER_Y - 1, STEPS):
-        send(s)
+    each(0, Z - 1, lambda k: copy_z(away(k), 3, relay).start())
+    beside = [copy_y(stage.at[2 * step_of(0, e // 2) + lax.rem(y + e % 2, 2)], 0, e) for e in range(1, Y)]
+    for copy in beside[1:]:
+        copy.start()
+    turn(Z)
+    turn_and_send(Z + 1, STEPS, 1)
+    each(0, Z - 1, lambda k: copy_z(away(k), 0, recv).start())
+    beside[0].start()
 
     wide = jnp.concatenate([hpair[...].astype(jnp.float32), jnp.zeros((RANK, 2 * MINE), jnp.float32)], axis=0)
     ht[...] = wide.T
     mine = pl.ds(pl.multiple_of(lax.rem(row, 2) * MINE, 8), MINE)
     high_t = ht[mine, :][:, 0:RANK].astype(jnp.bfloat16)
 
+    for copy in along_z:
+        copy.wait()
+    for copy in along_y:
+        copy.start()
+
+    def pass_on(dz, e):
+        copy_z(dz, e, relay).wait_recv()
+        copy_y(relay.at[dz * Y + e], dz, e).start()
+
+    each(0, Z - 1, lambda k: pass_on(away(k), 2))
+    for copy in along_y:
+        copy.wait()
+    for copy in aside:
+        copy.start()
+    each(0, Z - 1, lambda k: pass_on(away(k), 3))
     for copy in aside:
         copy.wait()
 
@@ -219,24 +223,40 @@
 
     norm_ref[...] = norms[...].astype(jnp.bfloat16)
 
-    @pl.loop(0, STEPS)
-    def _(s):
-        dz, q = step(s)
-
-        @pl.loop(0, 2)
-        def _(j):
-            away = dz + q + j > 0
-            from_z = lax.rem(z + Z - dz, Z)
-            from_y = partner(dz, q, j)[1]
-
-            @pl.when(away)
-            def _():
-                block_copy(s, j).wait()
-                add_block(recv[dz * Y + 2 * q + j], from_z, from_y)
-
-            @pl.when(jnp.logical_not(away))
-            def _():
-                add_block(stage[2 * s + lax.rem(y, 2)], z, y)
+    def add_from(dz, e):
+        add_block(recv[dz * Y + e], lax.rem(z + Z - dz, Z), partner(dz, e // 2, lax.rem(e, 2))[1])
+
+    def add_passed(dz, e):
+        copy_y(relay.at[dz * Y + e], dz, e).wait_recv()
+        add_from(dz, e)
+
+    def pass_and_add(k):
+        dz = away(k)
+        pass_on(dz, 1)
+        add_passed(dz, 2)
+        add_passed(dz, 3)
+
+    def add_last(k):
+        dz = away(k)
+        copy_z(dz, 0, recv).wait_recv()
+        add_from(dz, 0)
+
+    add_block(stage[2 * step_of(0, 0) + lax.rem(y, 2)], z, y)
+    each(1, Y, lambda e: add_passed(0, e))
+    each(0, Z - 1, pass_and_add)
+    each(0, Z - 1, lambda k: add_passed(away(k), 1))
+    each(0, Z - 1, add_last)
+
+    def sent_z(slot):
+        copy_z(slot // Y, lax.rem(slot, Y), recv).wait_send()
+
+    def sent_y(slot):
+        @pl.when(lax.rem(slot, Y) > 0)
+        def _():
+            copy_y(relay.at[slot], slot // Y, lax.rem(slot, Y)).wait_send()
+
+    each(Y, PLANE, sent_z)
+    each(0, PLANE, sent_y)
 
     scale = jnp.broadcast_to(jnp.sqrt(jnp.sum(acc[...], axis=1, keepdims=True)), (MINE, 128))
     inv_ref[...] = 1.0 / scale
@@ -278,6 +298,7 @@
             pltpu.VMEM((STEPS, ROWS, 2 * MINE), bf16),
             pltpu.VMEM((PLANE, MINE, ROWS), bf16),
             pltpu.VMEM((PLANE, MINE, ROWS), bf16),
+            pltpu.VMEM((PLANE, MINE, ROWS), bf16),
             pltpu.VMEM((C, X, Z, Y, 16, 256), bf16),
             pltpu.VMEM((X * C, 16, 128), bf16),
             pltpu.VMEM((RANK, 2 * MINE), bf16),
@@ -287,7 +308,7 @@
             pltpu.VMEM((RANK, ROWS), bf16),
             pltpu.VMEM((1, PIECE), f32),
             pltpu.VMEM((1, PIECE), f32),
-            dma((STEPS,)), dma((4,)), dma((PLANE,)), dma((PLANE,)),
+            dma((STEPS,)), dma((4,)), dma((PLANE,)), dma((PLANE,)), dma((PLANE,)), dma((PLANE,)),
             dma((X * C,)), dma((X * C,)), dma((hops,)), dma((hops,)),
         ],
         compiler_params=pltpu.CompilerParams(

time: 122 us -> 120 us (0.984)
  the two profiles are of different devices: /device:TPU:34 before, /device:TPU:9 now
where the time goes in v3:
time: 120 us; the launch traced here: 118 us
  Pallas kernels  118 us (98%)
    pallas_call x1, Pallas kernels, per_device(): pl.pallas_call(comm_kernel, out_shape=(pltpu.VMEM((MINE, D_MODEL), f32),...  115 us
    pallas_call x1, Pallas kernels, per_device(): pl.pallas_call(scale_kernel, grid=(WRITES,), out_shape=(jax.ShapeDtypeStr...  2.9 us

profile of v3, /device:TPU:9, one launch (start us, length us, event | category | flops | bytes accessed | tf_op | source)
XLA Modules:
  0.0 118.2 jit_solution(2634825385595996291)
XLA Ops:
  0.6 114.6 %exchange.1 = (f32[192,12288]{1,0:T(8,128)S(1)}, f32[192,128]{1,0:T(8,128)S(1)}, f32[8,256]{1,0:T(8,128)S(1)}, bf16[96,128]{1,0:T(8,128)(2,1)S(1)}) custom-call(bf16[384,6144]{1,0:T(8,128)(2,1)} %w_hbm.1, bf16[64,384]{1,0:T(8,128)(2,1)} %bitcast.6, bf16[64,6144]{1,0:T(8,128)(2,1)} %high_hbm.1, f32[1,48]{1,0:T(1,128)} %bitcast.7, f32[1,48]{1,0:T(1,128)} %bitcast.8), custom_call_target="tpu_custom_call" | custom-call | tf_op jit(solution)/shard_map/exchange/pallas_call | solution.py:287
  115.3 2.9 %rescale.1 = (bf16[192,12288]{1,0:T(8,128)(2,1)}, f32[1,192]{1,0:T(1,128)}, bf16[96,128]{1,0:T(8,128)(2,1)}) custom-call(f32[192,12288]{1,0:T(8,128)S(1)} %get-tuple-element.10.fresh_ref, f32[192,128]{1,0:T(8,128)S(1)} %get-tuple-element.11.inv_ref, f32[8,256]{1,0:T(8,128)S(1)} %get-tuple-element.12.scale_ref, bf16[96,128]{1,0:T(8,128)(2,1)S(1)} %get-tuple-element.13.norm_ref), custom_call_target="tpu_custom_call" | custom-call | tf_op jit(solution)/shard_map/rescale/pallas_call | solution.py:319

commit v4 on v3

--- a/solution.py
+++ b/solution.py
@@ -17,6 +17,8 @@
 MINE = COLS // PLANE
 PIECE = D_MODEL // (PLANE * X * C)
 STEPS = PLANE // 2
+AWAY = (5, 1, 6, 2, 7, 3, 4, 0)
+NEAR_FIRST = (7, 1, 6, 2, 5, 3, 4, 0)
 WRITES = 2
 
 mix_rate = 0.5
@@ -34,14 +36,21 @@
     me = x * C + c
 
     def step(s):
-        return away(lax.rem(s, Z)), 1 - s // Z
+        return away(s % Z if isinstance(s, int) else lax.rem(s, Z)), 1 - s // Z
 
     def step_of(dz, q):
-        k = lax.rem(dz + Z - 1, Z)
-        return 2 * lax.rem(k, Z // 2) + k // (Z // 2) + (1 - q) * Z
+        return listed(dz, [AWAY.index(k) for k in range(Z)]) + (1 - q) * Z
 
     def away(k):
-        return lax.rem(1 + k // 2 + Z // 2 * lax.rem(k, 2), Z)
+        return listed(k, AWAY)
+
+    def listed(k, table):
+        if isinstance(k, int):
+            return table[k]
+        found = jnp.int32(table[0])
+        for n in range(1, Z):
+            found = jnp.where(k == n, table[n], found)
+        return found
 
     def partner(dz, q, j):
         return lax.rem(z + dz, Z), 2 * lax.rem(y // 2 + q, 2) + lax.rem(y + j, 2)
@@ -117,7 +126,8 @@
     turn(0)
     turn(1)
     pl.semaphore_wait(barrier, Z - 1 + Y - 1 + X * C - 1)
-    copy_z(1, 2, relay).start()
+    copy_z(away(0), 2, relay).start()
+    turn_and_send(2, 4, 2)
 
     for copy in small:
         copy.wait()
@@ -147,7 +157,7 @@
 
     for k in range(1, X * C):
         gain_copy(k).start()
-    turn_and_send(2, Z, 2)
+    turn_and_send(4, Z, 2)
     for k in range(1, X * C):
         gain_copy(k).wait()
     gains = nbuf[0].astype(jnp.float32)
@@ -175,7 +185,10 @@
         copy.start()
     turn(Z)
     turn_and_send(Z + 1, STEPS, 1)
-    each(0, Z - 1, lambda k: copy_z(away(k), 0, recv).start())
+    def last_away(k):
+        return jnp.where(lax.rem(z + 1, Z) <= Z // 2, listed(k, NEAR_FIRST), listed(Z - 2 - k, NEAR_FIRST))
+
+    each(0, Z - 1, lambda k: copy_z(last_away(k), 0, recv).start())
     beside[0].start()
 
     wide = jnp.concatenate([hpair[...].astype(jnp.float32), jnp.zeros((RANK, 2 * MINE), jnp.float32)], axis=0)

time: 120 us -> 119 us (level)
  Pallas kernels: 118 us -> 116 us
    pallas_call x1, Pallas kernels: 115 us -> 113 us  [per_device(): pl.pallas_call(comm_kernel, out_shape=(pltpu.VMEM((MINE, D_MODEL), f32),...]
where the time goes in v4:
time: 119 us; the launch traced here: 117 us
  Pallas kernels  116 us (97%)
    pallas_call x1, Pallas kernels, per_device(): pl.pallas_call(comm_kernel, out_shape=(pltpu.VMEM((MINE, D_MODEL), f32),...  113 us
    pallas_call x1, Pallas kernels, per_device(): pl.pallas_call(scale_kernel, grid=(WRITES,), out_shape=(jax.ShapeDtypeStr...  2.9 us

profile of v4, /device:TPU:9, one launch (start us, length us, event | category | flops | bytes accessed | tf_op | source)
XLA Modules:
  0.0 116.7 jit_solution(13410295980339544947)
XLA Ops:
  0.6 113.2 %exchange.1 = (f32[192,12288]{1,0:T(8,128)S(1)}, f32[192,128]{1,0:T(8,128)S(1)}, f32[8,256]{1,0:T(8,128)S(1)}, bf16[96,128]{1,0:T(8,128)(2,1)S(1)}) custom-call(bf16[384,6144]{1,0:T(8,128)(2,1)} %w_hbm.1, bf16[64,384]{1,0:T(8,128)(2,1)} %bitcast.6, bf16[64,6144]{1,0:T(8,128)(2,1)} %high_hbm.1, f32[1,48]{1,0:T(1,128)} %bitcast.7, f32[1,48]{1,0:T(1,128)} %bitcast.8), custom_call_target="tpu_custom_call" | custom-call | tf_op jit(solution)/shard_map/exchange/pallas_call | solution.py:300
  113.8 2.9 %rescale.1 = (bf16[192,12288]{1,0:T(8,128)(2,1)}, f32[1,192]{1,0:T(1,128)}, bf16[96,128]{1,0:T(8,128)(2,1)}) custom-call(f32[192,12288]{1,0:T(8,128)S(1)} %get-tuple-element.10.fresh_ref, f32[192,128]{1,0:T(8,128)S(1)} %get-tuple-element.11.inv_ref, f32[8,256]{1,0:T(8,128)S(1)} %get-tuple-element.12.scale_ref, bf16[96,128]{1,0:T(8,128)(2,1)S(1)} %get-tuple-element.13.norm_ref), custom_call_target="tpu_custom_call" | custom-call | tf_op jit(solution)/shard_map/rescale/pallas_call | solution.py:332

commit v5 on v4

--- a/solution.py
+++ b/solution.py
@@ -258,18 +258,20 @@
     each(1, Y, lambda e: add_passed(0, e))
     each(0, Z - 1, pass_and_add)
     each(0, Z - 1, lambda k: add_passed(away(k), 1))
-    each(0, Z - 1, add_last)
-
-    def sent_z(slot):
-        copy_z(slot // Y, lax.rem(slot, Y), recv).wait_send()
-
-    def sent_y(slot):
+    def sent(slot):
         @pl.when(lax.rem(slot, Y) > 0)
         def _():
             copy_y(relay.at[slot], slot // Y, lax.rem(slot, Y)).wait_send()
 
-    each(Y, PLANE, sent_z)
-    each(0, PLANE, sent_y)
+            @pl.when(slot > Y)
+            def _():
+                copy_z(slot // Y, lax.rem(slot, Y), recv).wait_send()
+
+    each(0, PLANE, sent)
+    each(0, Z - 1, add_last)
+
+    for dz in range(1, Z):
+        copy_z(dz, 0, recv).wait_send()
 
     scale = jnp.broadcast_to(jnp.sqrt(jnp.sum(acc[...], axis=1, keepdims=True)), (MINE, 128))
     inv_ref[...] = 1.0 / scale

time: 119 us -> 118 us (level)
  no operation moved by 1% of the time
where the time goes in v5:
time: 118 us; the launch traced here: 116 us
  Pallas kernels  115 us (97%)
    pallas_call x1, Pallas kernels, per_device(): pl.pallas_call(comm_kernel, out_shape=(pltpu.VMEM((MINE, D_MODEL), f32),...  112 us
    pallas_call x1, Pallas kernels, per_device(): pl.pallas_call(scale_kernel, grid=(WRITES,), out_shape=(jax.ShapeDtypeStr...  2.9 us

profile of v5, /device:TPU:9, one launch (start us, length us, event | category | flops | bytes accessed | tf_op | source)
XLA Modules:
  0.0 115.9 jit_solution(3344573357957190944)
XLA Ops:
  0.6 112.4 %exchange.1 = (f32[192,12288]{1,0:T(8,128)S(1)}, f32[192,128]{1,0:T(8,128)S(1)}, f32[8,256]{1,0:T(8,128)S(1)}, bf16[96,128]{1,0:T(8,128)(2,1)S(1)}) custom-call(bf16[384,6144]{1,0:T(8,128)(2,1)} %w_hbm.1, bf16[64,384]{1,0:T(8,128)(2,1)} %bitcast.6, bf16[64,6144]{1,0:T(8,128)(2,1)} %high_hbm.1, f32[1,48]{1,0:T(1,128)} %bitcast.7, f32[1,48]{1,0:T(1,128)} %bitcast.8), custom_call_target="tpu_custom_call" | custom-call | tf_op jit(solution)/shard_map/exchange/pallas_call | solution.py:302
  113.0 2.9 %rescale.1 = (bf16[192,12288]{1,0:T(8,128)(2,1)}, f32[1,192]{1,0:T(1,128)}, bf16[96,128]{1,0:T(8,128)(2,1)}) custom-call(f32[192,12288]{1,0:T(8,128)S(1)} %get-tuple-element.10.fresh_ref, f32[192,128]{1,0:T(8,128)S(1)} %get-tuple-element.11.inv_ref, f32[8,256]{1,0:T(8,128)S(1)} %get-tuple-element.12.scale_ref, bf16[96,128]{1,0:T(8,128)(2,1)S(1)} %get-tuple-element.13.norm_ref), custom_call_target="tpu_custom_call" | custom-call | tf_op jit(solution)/shard_map/rescale/pallas_call | solution.py:334
